TPU v7x, 32 devices: a whole 2x2x4 slice. The times are simulated.
32 devices in a mesh: gx: 2 (over x), gy: 4 (over y, core), gz: 4 (over z).
Axes of the slice: x: 2, y: 2, z: 4, core: 2. Of those that a mesh axis runs over, the one named last changes fastest.
Arguments:
- ambient_motion_array: float32 [3, 16, 256, 512], P(None, 'gx', 'gy', 'gz'), may hold values from -6 to 6
- ambient_scalar_trio: float32 [3, 16, 256, 512], P(None, 'gx', 'gy', 'gz'), may hold values from 0.2 to 1
- droplet_local_position: float32 [3, 32768], P(None, ('gx', 'gy', 'gz')), may hold values from -0.5 to 0.5
- droplet_motion_array: float32 [3, 32768], P(None, ('gx', 'gy', 'gz')), may hold values from -6 to 6
- droplet_heat_level: float32 [32768], P(('gx', 'gy', 'gz')), may hold values from 0.3 to 0.9
- droplet_size_quadratic: float32 [32768], P(('gx', 'gy', 'gz')), may hold values from 0.25 to 4
- local_i_position: int32 [32768], P(('gx', 'gy', 'gz')), may hold values from 0 to 7
- local_j_position: int32 [32768], P(('gx', 'gy', 'gz')), may hold values from 0 to 63
- local_k_position: int32 [32768], P(('gx', 'gy', 'gz')), may hold values from 0 to 127
- active_group_tally: int32 [32], P(('gx', 'gy', 'gz')), may hold values from 1 to 8, as said below
Outputs:
- gas_source: float32 [5, 16, 256, 512], P(None, 'gx', 'gy', 'gz')
- parcel_state: float32 [5, 32768], P(None, ('gx', 'gy', 'gz'))
Inputs may be any that keep to these rules, and one draw needn't show every extreme that they name: `active_group_tally`: tiles of a brick are live from the first one on; in every draw some brick has all 8 tiles live.
All inputs are finite; a program needn't handle non-finite values.
Results may differ from a plain program's by a relative error of at most 0.0003.
Values sent between devices are 32-bit elements; how exact they have to be, the bound alone decides.
A program may use at most 128 MiB of HBM per device.

v0:
```python
import functools

import jax
import jax.numpy as jnp
from jax import lax
from jax.experimental import pallas as pl
from jax.experimental.pallas import tpu as pltpu
from jax.sharding import PartitionSpec as P

TILE = 128
AXES = ("gx", "gy", "gz")
MESH = pl.DeviceIdType.MESH
F32 = jnp.float32
BF16 = jnp.bfloat16

step_time = 0.25
evap_rate = 1.0
heat_rate = 2.0
boiling_energy_drain = 0.3

X_MOVES = ((1, 0, 0, 0), (-1, 0, 0, 1))
Y_MOVES = ((0, 1, 0, 0), (0, -1, 0, 1))
XY_MOVES = ((1, 1, 0, 0), (1, -1, 0, 1), (-1, 1, 0, 2), (-1, -1, 0, 3))
Z_MOVES = ((0, 0, 1, 0), (0, 0, -1, 1))


def split(value):
    high = value.astype(BF16)
    return high, (value - high.astype(F32)).astype(BF16)


def nn(a, b):
    return lax.dot_general(a, b, (((1,), (0,)), ((), ())), preferred_element_type=F32)


def nt(a, b):
    return lax.dot_general(a, b, (((1,), (1,)), ((), ())), preferred_element_type=F32)


def tn(a, b):
    return lax.dot_general(a, b, (((0,), (0,)), ((), ())), preferred_element_type=F32)


def pair_weights(offset):
    lower = jnp.where(offset < 0.0, -1.0, 0.0)
    first = jnp.maximum(0.0, 1.0 - jnp.abs(offset - lower))
    second = jnp.maximum(0.0, 1.0 - jnp.abs(offset - (lower + 1.0)))
    return first, second, jnp.where(offset < 0.0, -1, 0)


def kernel(
    counts,
    vel,
    sca,
    pos,
    mot,
    heat,
    size,
    li,
    lj,
    lk,
    tally,
    dep,
    state,
    fields,
    ft_hi,
    ft_lo,
    w_hi,
    w_lo,
    line,
    src_hi,
    src_lo,
    sampled,
    xh,
    yh,
    xyh,
    zh,
    ys,
    xys,
    zs,
    dxs,
    dys,
    dxys,
    dzs,
    dxr,
    dyr,
    dxyr,
    dzr,
    load_sem,
    send_sem,
    recv_sem,
):
    ci, cj, ck = vel.shape[1:]
    slots = heat.shape[1]
    inner = ci * cj
    planes = w_hi.shape[0]
    outer = planes - inner
    y_row = 2 * cj
    xy_row = y_row + 2 * ci
    me = [lax.axis_index(axis) for axis in AXES]

    def exists(move, sign):
        good = None
        for d in range(3):
            step = sign * move[d]
            if step == 1:
                test = me[d] < counts[d] - 1
            elif step == -1:
                test = me[d] > 0
            else:
                continue
            good = test if good is None else jnp.logical_and(good, test)
        return good

    def peer(move):
        return tuple(lax.rem(me[d] + move[d] + counts[d], counts[d]) for d in range(3))

    moves = X_MOVES + Y_MOVES + XY_MOVES + Z_MOVES

    class Message:
        def __init__(self, number, move, src, dst):
            self.move = move
            self.dst = dst
            self.copy = pltpu.make_async_remote_copy(
                src_ref=src,
                dst_ref=dst,
                send_sem=send_sem.at[number],
                recv_sem=recv_sem.at[number],
                device_id=peer(move),
                device_id_type=MESH,
            )

        def start(self):
            @pl.when(exists(self.move, 1))
            def _():
                self.copy.start()

        def blank(self):
            @pl.when(jnp.logical_not(exists(self.move, -1)))
            def _():
                self.dst[...] = jnp.zeros(self.dst.shape, F32)

        def arrive(self):
            @pl.when(exists(self.move, -1))
            def _():
                self.copy.wait_recv()

        def leave(self):
            @pl.when(exists(self.move, 1))
            def _():
                self.copy.wait_send()

    x_in, y_in, z_in, x_out, xy_out, z_out = [], [], [], [], [], []
    number = 0

    def add(group, move, src, dst):
        nonlocal number
        group.append(Message(number, move, src, dst))
        number += 1

    for move in X_MOVES:
        row = ci - 1 if move[0] > 0 else 0
        add(x_in, move, vel.at[:, row], xh.at[move[3], 0:3])
        add(x_in, move, sca.at[:, row], xh.at[move[3], 3:6])
    for move in Y_MOVES:
        add(y_in, move, ys.at[move[3]], yh.at[move[3]])
    for move in XY_MOVES:
        add(y_in, move, xys.at[move[3]], xyh.at[move[3]])
    for move in Z_MOVES:
        add(z_in, move, zs.at[move[3]], zh.at[move[3]])
    for move in Z_MOVES:
        add(z_out, move, dzs.at[move[3]], dzr.at[move[3]])
    for move in X_MOVES:
        add(x_out, move, dxs.at[move[3]], dxr.at[move[3]])
    for move in Y_MOVES:
        add(xy_out, move, dys.at[move[3]], dyr.at[move[3]])
    for move in XY_MOVES:
        add(xy_out, move, dxys.at[move[3]], dxyr.at[move[3]])

    barrier = pltpu.get_barrier_semaphore()
    for move in moves:

        @pl.when(exists(move, 1))
        def _():
            pl.semaphore_signal(barrier, inc=1, device_id=peer(move), device_id_type=MESH)

    loads = [
        pltpu.make_async_copy(vel, fields.at[0:3], load_sem.at[0]),
        pltpu.make_async_copy(sca, fields.at[3:6], load_sem.at[1]),
    ]
    for load in loads:
        load.start()
    for message in x_in + y_in + z_in + z_out + x_out + xy_out:
        message.blank()

    pl.semaphore_wait(barrier, sum(exists(move, 1).astype(jnp.int32) for move in moves))

    for message in x_in:
        message.start()
    for load in loads:
        load.wait()

    for s in range(2):
        row = cj - 1 if s == 0 else 0
        ys[s] = fields[:, :, row, :]
        for t in range(2):
            plane = ci - 1 if t == 0 else 0
            xys[t * 2 + s] = jnp.concatenate(
                [fields[:, plane, row, :], jnp.zeros((2, ck), F32)], axis=0
            )
    for message in y_in:
        message.start()

    xa, xb, lx = pair_weights(pos[0:1])
    ya, yb, ly = pair_weights(pos[1:2])
    za, zb, lz = pair_weights(pos[2:3])
    i0 = li[...] + lx
    j0 = lj[...] + ly
    k0 = lk[...] + lz
    codes = []
    for a, wa in enumerate((xa, xb)):
        for b, wb in enumerate((ya, yb)):
            i, j = i0 + a, j0 + b
            out_i = (i < 0) | (i >= ci)
            out_j = (j < 0) | (j >= cj)
            si = jnp.where(i < 0, 0, 1)
            sj = jnp.where(j < 0, 0, 1)
            code = jnp.where(
                out_i,
                jnp.where(out_j, inner + xy_row + si * 2 + sj, inner + si * cj + j),
                jnp.where(out_j, inner + y_row + sj * ci + i, i * cj + j),
            )
            codes.append((code, wa * wb))
    block = 128
    for start in range(0, planes, block):
        rows = lax.broadcasted_iota(jnp.int32, (block, slots), 0) + start
        table = jnp.zeros((block, slots), F32)
        for code, weight in codes:
            table = jnp.where(rows == code, weight, table)
        high, low = split(table)
        w_hi[start : start + block] = high
        w_lo[start : start + block] = low
    lines = lax.broadcasted_iota(jnp.int32, (ck, slots), 0)
    line[...] = jnp.where(lines == k0, za, jnp.where(lines == k0 + 1, zb, 0.0))
    rim = (jnp.where(k0 < 0, za, 0.0), jnp.where(k0 + 1 >= ck, zb, 0.0))

    zs[...] = jnp.zeros_like(zs)

    def lay(f, first, flat):
        wide = flat.shape[0]
        turned = flat.T
        high, low = split(turned)
        ft_hi[f * ck : (f + 1) * ck, first : first + wide] = high
        ft_lo[f * ck : (f + 1) * ck, first : first + wide] = low
        zs[0, f : f + 1, first : first + wide] = turned[ck - 1 : ck]
        zs[1, f : f + 1, first : first + wide] = turned[0:1]

    for f in range(6):
        lay(f, 0, fields[f].reshape(inner, ck))

    width = 256

    def sample(first, last, fresh):
        for s in range(0, slots, width):
            here = slice(s, s + width)
            got = nn(ft_hi[:, first:last], w_hi[first:last, here])
            got += nn(ft_hi[:, first:last], w_lo[first:last, here])
            got += nn(ft_lo[:, first:last], w_hi[first:last, here])
            for f in range(6):
                part = jnp.sum(
                    got[f * ck : (f + 1) * ck] * line[:, here], axis=0, keepdims=True
                )
                if fresh:
                    sampled[f : f + 1, here] = part
                else:
                    sampled[f : f + 1, here] += part

    sample(0, inner, True)

    for message in x_in + y_in:
        message.arrive()
    for f in range(6):
        flat = jnp.concatenate(
            [xh[0, f], xh[1, f], yh[0, f], yh[1, f]]
            + [xyh[q, f : f + 1] for q in range(4)]
            + [jnp.zeros((outer - xy_row - 4, ck), F32)],
            axis=0,
        )
        lay(f, inner, flat)
    for message in z_in:
        message.start()
    sample(inner, planes, False)
    for message in z_in:
        message.arrive()
    ends = jnp.concatenate([zh[0], zh[1]], axis=0)
    end_hi, end_lo = split(ends)
    got = nn(end_hi, w_hi[...]) + nn(end_hi, w_lo[...]) + nn(end_lo, w_hi[...])
    gas = sampled[...] + got[0:8] * rim[0] + got[8:16] * rim[1]

    live = lax.broadcasted_iota(jnp.int32, (1, slots), 1) // TILE < tally[0]
    q = size[...]
    tp = heat[...]
    v = mot[...]
    drag = step_time / (0.5 * q)
    v_new = (v + drag * gas[0:3]) / (1.0 + drag)
    mass = q * jnp.sqrt(q)
    share = jnp.exp(4.0 * (tp - 1.0))
    decay = step_time * evap_rate * gas[5:6] * (share - gas[4:5])
    q_new = q - decay
    mass_new = q_new * jnp.sqrt(q_new)
    conduct = step_time * heat_rate * gas[5:6] / q
    tp_new = (tp + conduct * gas[3:4]) / (1.0 + conduct) - boiling_energy_drain * decay / q
    state[0:3] = jnp.where(live, v_new, v)
    state[3:4] = jnp.where(live, tp_new, tp)
    state[4:5] = jnp.where(live, q_new, q)
    push = jnp.where(live, mass * (v - v_new), 0.0)
    terms = [
        push[0:1],
        push[1:2],
        push[2:3],
        jnp.where(live, mass * (tp - tp_new), 0.0),
        jnp.where(live, mass - mass_new, 0.0),
    ]
    stack = jnp.concatenate(terms + [jnp.zeros((3, slots), F32)], axis=0)
    ends = jnp.concatenate([stack * rim[1], stack * rim[0]], axis=0)
    end_hi, end_lo = split(ends)
    got = nt(end_hi, w_hi[...]) + nt(end_hi, w_lo[...]) + nt(end_lo, w_hi[...])
    dzs[0] = got[0:8]
    dzs[1] = got[8:16]
    for message in z_out:
        message.start()

    for c in range(5):
        high, low = split(line[...] * terms[c])
        src_hi[c * ck : (c + 1) * ck] = high
        src_lo[c * ck : (c + 1) * ck] = low

    def spread(first, last, low, high):
        got = nt(w_hi[first:last], src_hi[low:high])
        got += nt(w_hi[first:last], src_lo[low:high])
        got += nt(w_lo[first:last], src_hi[low:high])
        return got

    pick_row = lax.broadcasted_iota(jnp.int32, (32, 5 * ck), 0)
    pick_col = lax.broadcasted_iota(jnp.int32, (32, 5 * ck), 1)
    pick_row = jnp.where(pick_row >= 16, pick_row - 16, pick_row)
    target = jnp.where(pick_row >= 8, (pick_row - 8) * ck + ck - 1, pick_row * ck)
    pick = jnp.where(target == pick_col, 1.0, 0.0).astype(BF16)

    spans = [(c, min(c + 2, 5)) for c in range(0, 5, 2)]
    halo = [spread(inner, planes, a * ck, b * ck) for a, b in spans]
    for message in z_out:
        message.arrive()
    ends = jnp.concatenate([dzr[0], dzr[1]], axis=0)
    end_hi, end_lo = split(ends)
    ends = jnp.concatenate([end_hi, end_lo], axis=0)
    for part, (a, b) in zip(halo, spans):
        part = part + tn(ends[:, inner:], pick[:, a * ck : b * ck])
        for c in range(a, b):
            piece = part[:, (c - a) * ck : (c - a + 1) * ck]
            dxs[1, c] = piece[0:cj]
            dxs[0, c] = piece[cj : 2 * cj]
            dys[1, c] = piece[y_row : y_row + ci]
            dys[0, c] = piece[y_row + ci : y_row + 2 * ci]
            for n in range(4):
                dxys[3 - n, c : c + 1] = piece[xy_row + n : xy_row + n + 1]
    for message in x_out + xy_out:
        message.start()

    for a, b in spans:
        part = spread(0, inner, a * ck, b * ck) + tn(ends[:, :inner], pick[:, a * ck : b * ck])
        for c in range(a, b):
            dep[c] = part[:, (c - a) * ck : (c - a + 1) * ck].reshape(ci, cj, ck)

    for message in x_out + xy_out:
        message.arrive()
    for s in range(2):
        plane = 0 if s == 0 else ci - 1
        dep[:, plane] += dxr[s]
    for s in range(2):
        row = 0 if s == 0 else cj - 1
        dep[:, :, row, :] += dyr[s]
        for t in range(2):
            plane = 0 if t == 0 else ci - 1
            dep[:, plane, row, :] += dxyr[t * 2 + s, 0:5]
    for message in x_in + y_in + z_in + z_out + x_out + xy_out:
        message.leave()


def local(counts, vel, sca, pos, mot, heat, size, li, lj, lk, tally):
    ci, cj, ck = vel.shape[1:]
    slots = heat.shape[0]
    outer = 2 * cj + 2 * ci + 4
    planes = ci * cj + -(-outer // 128) * 128
    vmem = pl.BlockSpec(memory_space=pltpu.VMEM)
    row = lambda value: value.reshape(1, slots)
    messages = 24
    scratch = [
        pltpu.VMEM((6, ci, cj, ck), F32),
        pltpu.VMEM((6 * ck, planes), BF16),
        pltpu.VMEM((6 * ck, planes), BF16),
        pltpu.VMEM((planes, slots), BF16),
        pltpu.VMEM((planes, slots), BF16),
        pltpu.VMEM((ck, slots), F32),
        pltpu.VMEM((5 * ck, slots), BF16),
        pltpu.VMEM((5 * ck, slots), BF16),
        pltpu.VMEM((8, slots), F32),
        pltpu.VMEM((2, 6, cj, ck), F32),
        pltpu.VMEM((2, 6, ci, ck), F32),
        pltpu.VMEM((4, 8, ck), F32),
        pltpu.VMEM((2, 8, planes), F32),
        pltpu.VMEM((2, 6, ci, ck), F32),
        pltpu.VMEM((4, 8, ck), F32),
        pltpu.VMEM((2, 8, planes), F32),
        pltpu.VMEM((2, 5, cj, ck), F32),
        pltpu.VMEM((2, 5, ci, ck), F32),
        pltpu.VMEM((4, 8, ck), F32),
        pltpu.VMEM((2, 8, planes), F32),
        pltpu.VMEM((2, 5, cj, ck), F32),
        pltpu.VMEM((2, 5, ci, ck), F32),
        pltpu.VMEM((4, 8, ck), F32),
        pltpu.VMEM((2, 8, planes), F32),
        pltpu.SemaphoreType.DMA((2,)),
        pltpu.SemaphoreType.DMA((messages,)),
        pltpu.SemaphoreType.DMA((messages,)),
    ]
    return pl.pallas_call(
        functools.partial(kernel, counts),
        out_shape=(
            jax.ShapeDtypeStruct((5, ci, cj, ck), F32),
            jax.ShapeDtypeStruct((5, slots), F32),
        ),
        in_specs=[pl.BlockSpec(memory_space=pl.ANY)] * 2
        + [vmem] * 7
        + [pl.BlockSpec(memory_space=pltpu.SMEM)],
        out_specs=(vmem, vmem),
        scratch_shapes=scratch,
        compiler_params=pltpu.CompilerParams(collective_id=0, has_side_effects=True),
    )(vel, sca, pos, mot, row(heat), row(size), row(li), row(lj), row(lk), tally)


def solution(mesh):
    bricks = P(None, AXES[0], AXES[1], AXES[2])
    rows = P(None, AXES)
    flat = P(AXES)
    counts = tuple(mesh.shape[axis] for axis in AXES)
    return jax.shard_map(
        functools.partial(local, counts),
        mesh=mesh,
        in_specs=(bricks, bricks, rows, rows) + (flat,) * 6,
        out_specs=(bricks, rows),
        check_vma=False,
    )
```

profile of v0, /device:TPU:1, one launch (start us, length us, event | category | flops | bytes accessed | tf_op | source)
XLA Modules:
  0.0 31.4 jit_solution(15886225970248765965)
XLA Ops:
  1.3 27.0 %shard_map.113 = (f32[5,8,64,128]{3,2,1,0:T(8,128)}, f32[5,1024]{1,0:T(8,128)}) custom-call(f32[3,8,64,128]{3,2,1,0:T(8,128)} %vel.1, f32[3,8,64,128]{3,2,1,0:T(8,128)} %sca.1, f32[3,1024]{1,0:T(4,128)} %pos.1, f32[3,1024]{1,0:T(4,128)} %mot.1, f32[1,1024]{1,0:T(1,128)} %bitcast.5, f32[1,1024]{1,0:T(1,128)} %bitcast.6, s32[1,1024]{1,0:T(1,128)} %bitcast.7, ...), custom_call_target="tpu_custom_call" | custom-call | tf_op jit(solution)/shard_map/pallas_call | solution.py:427
  28.3 0.0 copy-start
  28.3 2.5 %copy.15 = f32[5,8,64,128]{3,2,1,0:T(8,128)} copy(f32[5,8,64,128]{3,2,1,0:T(8,128)} %get-tuple-element.4) | data formatting | bytes 2621440
  30.8 0.0 copy-done
  30.8 0.6 %copy.16 = f32[5,1024]{1,0:T(8,128)} copy(f32[5,1024]{1,0:T(8,128)S(1)} %copy-done) | data formatting | bytes 40960
Async XLA Ops:
  28.3 2.5 %copy-start = (f32[5,1024]{1,0:T(8,128)S(1)}, f32[5,1024]{1,0:T(8,128)}, u32[]{:S(2)}) copy-start(f32[5,1024]{1,0:T(8,128)} %get-tuple-element.5) | copy-start | bytes 61444
where the time goes:
time: 31.7 us; the launch traced here: 31.4 us
  Pallas kernels  27 us (85%)
  local copies, waits for them, and re-layouts  3.15 us (10%)
  between operations  1.3 us (4%)
    pallas_call x1, Pallas kernels, local(): pl.pallas_call(functools.partial(kernel, counts), out_shape=(jax.ShapeDty...  27 us
    unnamed x4, local copies, waits for them, and re-layouts  3.15 us

commit v1 on v0

--- a/solution.py
+++ b/solution.py
@@ -52,6 +52,16 @@
     counts,
     vel,
     sca,
+    pos_in,
+    mot_in,
+    heat_in,
+    size_in,
+    li_in,
+    lj_in,
+    lk_in,
+    tally,
+    dep,
+    state,
     pos,
     mot,
     heat,
@@ -59,12 +69,8 @@
     li,
     lj,
     lk,
-    tally,
-    dep,
-    state,
     fields,
-    ft_hi,
-    ft_lo,
+    ft,
     w_hi,
     w_lo,
     line,
@@ -91,7 +97,7 @@
     recv_sem,
 ):
     ci, cj, ck = vel.shape[1:]
-    slots = heat.shape[1]
+    slots = heat_in.shape[1]
     inner = ci * cj
     planes = w_hi.shape[0]
     outer = planes - inner
@@ -188,28 +194,18 @@
         pltpu.make_async_copy(vel, fields.at[0:3], load_sem.at[0]),
         pltpu.make_async_copy(sca, fields.at[3:6], load_sem.at[1]),
     ]
-    for load in loads:
+    pairs = ((pos_in, pos), (li_in, li), (lj_in, lj), (lk_in, lk))
+    pairs += ((mot_in, mot), (heat_in, heat), (size_in, size))
+    smalls = [
+        pltpu.make_async_copy(a, b, load_sem.at[2 + n]) for n, (a, b) in enumerate(pairs)
+    ]
+    for load in smalls + loads:
         load.start()
     for message in x_in + y_in + z_in + z_out + x_out + xy_out:
         message.blank()
 
-    pl.semaphore_wait(barrier, sum(exists(move, 1).astype(jnp.int32) for move in moves))
-
-    for message in x_in:
-        message.start()
-    for load in loads:
+    for load in smalls:
         load.wait()
-
-    for s in range(2):
-        row = cj - 1 if s == 0 else 0
-        ys[s] = fields[:, :, row, :]
-        for t in range(2):
-            plane = ci - 1 if t == 0 else 0
-            xys[t * 2 + s] = jnp.concatenate(
-                [fields[:, plane, row, :], jnp.zeros((2, ck), F32)], axis=0
-            )
-    for message in y_in:
-        message.start()
 
     xa, xb, lx = pair_weights(pos[0:1])
     ya, yb, ly = pair_weights(pos[1:2])
@@ -244,14 +240,32 @@
     line[...] = jnp.where(lines == k0, za, jnp.where(lines == k0 + 1, zb, 0.0))
     rim = (jnp.where(k0 < 0, za, 0.0), jnp.where(k0 + 1 >= ck, zb, 0.0))
 
+    pl.semaphore_wait(barrier, sum(exists(move, 1).astype(jnp.int32) for move in moves))
+
+    for message in x_in:
+        message.start()
+    for load in loads:
+        load.wait()
+
+    for s in range(2):
+        row = cj - 1 if s == 0 else 0
+        ys[s] = fields[:, :, row, :]
+        for t in range(2):
+            plane = ci - 1 if t == 0 else 0
+            xys[t * 2 + s] = jnp.concatenate(
+                [fields[:, plane, row, :], jnp.zeros((2, ck), F32)], axis=0
+            )
+    for message in y_in:
+        message.start()
+
     zs[...] = jnp.zeros_like(zs)
 
     def lay(f, first, flat):
         wide = flat.shape[0]
         turned = flat.T
         high, low = split(turned)
-        ft_hi[f * ck : (f + 1) * ck, first : first + wide] = high
-        ft_lo[f * ck : (f + 1) * ck, first : first + wide] = low
+        ft[f * ck : (f + 1) * ck, first : first + wide] = high
+        ft[(6 + f) * ck : (7 + f) * ck, first : first + wide] = low
         zs[0, f : f + 1, first : first + wide] = turned[ck - 1 : ck]
         zs[1, f : f + 1, first : first + wide] = turned[0:1]
 
@@ -263,9 +277,9 @@
     def sample(first, last, fresh):
         for s in range(0, slots, width):
             here = slice(s, s + width)
-            got = nn(ft_hi[:, first:last], w_hi[first:last, here])
-            got += nn(ft_hi[:, first:last], w_lo[first:last, here])
-            got += nn(ft_lo[:, first:last], w_hi[first:last, here])
+            both = nn(ft[:, first:last], w_hi[first:last, here])
+            got = both[: 6 * ck] + both[6 * ck :]
+            got += nn(ft[: 6 * ck, first:last], w_lo[first:last, here])
             for f in range(6):
                 part = jnp.sum(
                     got[f * ck : (f + 1) * ck] * line[:, here], axis=0, keepdims=True
@@ -294,7 +308,8 @@
         message.arrive()
     ends = jnp.concatenate([zh[0], zh[1]], axis=0)
     end_hi, end_lo = split(ends)
-    got = nn(end_hi, w_hi[...]) + nn(end_hi, w_lo[...]) + nn(end_lo, w_hi[...])
+    both = nn(jnp.concatenate([end_hi, end_lo], axis=0), w_hi[...])
+    got = both[0:16] + both[16:32] + nn(end_hi, w_lo[...])
     gas = sampled[...] + got[0:8] * rim[0] + got[8:16] * rim[1]
 
     live = lax.broadcasted_iota(jnp.int32, (1, slots), 1) // TILE < tally[0]
@@ -323,14 +338,10 @@
     ]
     stack = jnp.concatenate(terms + [jnp.zeros((3, slots), F32)], axis=0)
     ends = jnp.concatenate([stack * rim[1], stack * rim[0]], axis=0)
-    end_hi, end_lo = split(ends)
-    got = nt(end_hi, w_hi[...]) + nt(end_hi, w_lo[...]) + nt(end_lo, w_hi[...])
-    dzs[0] = got[0:8]
-    dzs[1] = got[8:16]
-    for message in z_out:
-        message.start()
-
-    for c in range(5):
+    high, low = split(ends)
+    src_hi[5 * ck : 5 * ck + 16] = high
+    src_lo[5 * ck : 5 * ck + 16] = low
+    for c in (4, 0, 1, 2, 3):
         high, low = split(line[...] * terms[c])
         src_hi[c * ck : (c + 1) * ck] = high
         src_lo[c * ck : (c + 1) * ck] = low
@@ -347,8 +358,15 @@
     target = jnp.where(pick_row >= 8, (pick_row - 8) * ck + ck - 1, pick_row * ck)
     pick = jnp.where(target == pick_col, 1.0, 0.0).astype(BF16)
 
-    spans = [(c, min(c + 2, 5)) for c in range(0, 5, 2)]
-    halo = [spread(inner, planes, a * ck, b * ck) for a, b in spans]
+    spans = ((0, 2), (2, 4), (4, 5))
+    tail = spread(0, planes, 4 * ck, 5 * ck + 16)
+    turned = tail[:, ck:].T
+    dzs[0] = turned[0:8]
+    dzs[1] = turned[8:16]
+    for message in z_out:
+        message.start()
+    halo = [spread(inner, planes, a * ck, b * ck) for a, b in spans[:2]]
+    halo.append(tail[inner:, :ck])
     for message in z_out:
         message.arrive()
     ends = jnp.concatenate([dzr[0], dzr[1]], axis=0)
@@ -367,8 +385,9 @@
     for message in x_out + xy_out:
         message.start()
 
-    for a, b in spans:
-        part = spread(0, inner, a * ck, b * ck) + tn(ends[:, :inner], pick[:, a * ck : b * ck])
+    for a, b in spans[::-1]:
+        part = tail[:inner, :ck] if a == 4 else spread(0, inner, a * ck, b * ck)
+        part = part + tn(ends[:, :inner], pick[:, a * ck : b * ck])
         for c in range(a, b):
             dep[c] = part[:, (c - a) * ck : (c - a + 1) * ck].reshape(ci, cj, ck)
 
@@ -395,15 +414,16 @@
     vmem = pl.BlockSpec(memory_space=pltpu.VMEM)
     row = lambda value: value.reshape(1, slots)
     messages = 24
-    scratch = [
+    scratch = [pltpu.VMEM((3, slots), F32)] * 2 + [pltpu.VMEM((1, slots), F32)] * 2
+    scratch += [pltpu.VMEM((1, slots), jnp.int32)] * 3
+    scratch += [
         pltpu.VMEM((6, ci, cj, ck), F32),
-        pltpu.VMEM((6 * ck, planes), BF16),
-        pltpu.VMEM((6 * ck, planes), BF16),
+        pltpu.VMEM((12 * ck, planes), BF16),
         pltpu.VMEM((planes, slots), BF16),
         pltpu.VMEM((planes, slots), BF16),
         pltpu.VMEM((ck, slots), F32),
-        pltpu.VMEM((5 * ck, slots), BF16),
-        pltpu.VMEM((5 * ck, slots), BF16),
+        pltpu.VMEM((5 * ck + 16, slots), BF16),
+        pltpu.VMEM((5 * ck + 16, slots), BF16),
         pltpu.VMEM((8, slots), F32),
         pltpu.VMEM((2, 6, cj, ck), F32),
         pltpu.VMEM((2, 6, ci, ck), F32),
@@ -420,7 +440,7 @@
         pltpu.VMEM((2, 5, ci, ck), F32),
         pltpu.VMEM((4, 8, ck), F32),
         pltpu.VMEM((2, 8, planes), F32),
-        pltpu.SemaphoreType.DMA((2,)),
+        pltpu.SemaphoreType.DMA((9,)),
         pltpu.SemaphoreType.DMA((messages,)),
         pltpu.SemaphoreType.DMA((messages,)),
     ]
@@ -430,8 +450,7 @@
             jax.ShapeDtypeStruct((5, ci, cj, ck), F32),
             jax.ShapeDtypeStruct((5, slots), F32),
         ),
-        in_specs=[pl.BlockSpec(memory_space=pl.ANY)] * 2
-        + [vmem] * 7
+        in_specs=[pl.BlockSpec(memory_space=pltpu.HBM)] * 9
         + [pl.BlockSpec(memory_space=pltpu.SMEM)],
         out_specs=(vmem, vmem),
         scratch_shapes=scratch,

time: 31.7 us -> 32.3 us (1.019)
  Pallas kernels: 27 us -> 27.6 us
    pallas_call x1, Pallas kernels: 27 us -> 27.6 us  [local(): pl.pallas_call(functools.partial(kernel, counts), out_shape=(jax.ShapeDty...]
where the time goes in v1:
time: 32.3 us; the launch traced here: 32 us
  Pallas kernels  27.6 us (85%)
  local copies, waits for them, and re-layouts  3.15 us (10%)
  between operations  1.3 us (4%)
    pallas_call x1, Pallas kernels, local(): pl.pallas_call(functools.partial(kernel, counts), out_shape=(jax.ShapeDty...  27.6 us
    unnamed x4, local copies, waits for them, and re-layouts  3.15 us

profile of v1, /device:TPU:1, one launch (start us, length us, event | category | flops | bytes accessed | tf_op | source)
XLA Modules:
  0.0 32.0 jit_solution(6414686984587540135)
XLA Ops:
  1.3 27.6 %shard_map.113 = (f32[5,8,64,128]{3,2,1,0:T(8,128)}, f32[5,1024]{1,0:T(8,128)}) custom-call(f32[3,8,64,128]{3,2,1,0:T(8,128)} %vel.1, f32[3,8,64,128]{3,2,1,0:T(8,128)} %sca.1, f32[3,1024]{1,0:T(4,128)} %pos_in.1, f32[3,1024]{1,0:T(4,128)} %mot_in.1, f32[1,1024]{1,0:T(1,128)} %bitcast.5, f32[1,1024]{1,0:T(1,128)} %bitcast.6, s32[1,1024]{1,0:T(1,128)} %bitcast.7, ...), custom_call_target="tpu_custom_call" | custom-call | tf_op jit(solution)/shard_map/pallas_call | solution.py:447
  28.9 0.0 copy-start
  28.9 2.5 %copy.15 = f32[5,8,64,128]{3,2,1,0:T(8,128)} copy(f32[5,8,64,128]{3,2,1,0:T(8,128)} %get-tuple-element.4) | data formatting | bytes 2621440
  31.4 0.0 copy-done
  31.4 0.6 %copy.16 = f32[5,1024]{1,0:T(8,128)} copy(f32[5,1024]{1,0:T(8,128)S(1)} %copy-done) | data formatting | bytes 40960
Async XLA Ops:
  28.9 2.5 %copy-start = (f32[5,1024]{1,0:T(8,128)S(1)}, f32[5,1024]{1,0:T(8,128)}, u32[]{:S(2)}) copy-start(f32[5,1024]{1,0:T(8,128)} %get-tuple-element.5) | copy-start | bytes 61444
